TPU v7x, 256 devices: a whole 4x4x8 slice. The times are simulated.
256 devices in a mesh: team: 8 (over x, core), row: 2 (over z_hi), col: 16 (over y, z_lo).
Axes of the slice: x: 4, y: 4, z: 8 (z_hi: 2, z_lo: 4; z = z_hi * 4 + z_lo), core: 2. Of those that a mesh axis runs over, the one named last changes fastest.
Arguments:
- old_tiles: bfloat16 [8, 768, 256, 256], P('team', ('row', 'col')), may hold values from -4 to 4
- remap: int32 [8, 768], P('team', ('row', 'col')), may hold values from 0 to 255, as said below
- pivot_cols: bfloat16 [8, 5120, 1024], P('team', ('row', 'col')), may hold values from -6 to 6
- pivot_order: int32 [8, 2, 512], P('team'), may hold values from 0 to 511, each once within a row
- pivot_pattern: int32 [8, 2, 256], P('team'), may hold values 0 or 1
- block_inverses: float32 [8, 2, 3, 256], P('team'), may hold values from -0.05 to 0.05
- delays: int32 [8, 2], P('team'), may hold values from 0 to 128
Outputs:
- parent: float32 [2, 2048, 4096], P('row', 'team', 'col')
- second_panel: float32 [8, 5120, 512], P('team', ('row', 'col'))
Inputs may be any that keep to these rules, and one draw needn't show every extreme that they name: `remap`: tiles that one device holds go to at most 12 distinct owners, the owner of tile (i, j) being the device at row i // 8, column j; at most 2 of one device's tiles go to one owner, and in every front some owner receives exactly 2 tiles from every device.
All inputs are finite; a program needn't handle non-finite values. No bound on the sum of `pivot_pattern` on one device may be relied on, other than what follows from the above.
Results may differ from a plain program's by a relative error of at most 0.0003.
Values may be sent and summed in bfloat16 or wider, within the bound.
A program may use at most 128 MiB of HBM per device.

v0:
```python
import jax
import jax.numpy as jnp
from jax import lax
from jax.sharding import Mesh
from jax.sharding import PartitionSpec as P

COL = ("col_0", "col_1")
ROW_COL = ("row", "col_0", "col_1")


def laid_out(pieces, dim):
    shape = list(pieces.shape[1:])
    shape[dim] *= pieces.shape[0]
    return jnp.moveaxis(pieces, 0, dim).reshape(shape)


def all_blocks(shard, axes, sequence):
    pieces = shard[None]
    for k in sequence:
        pieces = lax.all_gather(pieces, axes[k], axis=0, tiled=True)
    current = [lax.axis_size(axes[k]) for k in reversed(sequence)]
    pieces = pieces.reshape(*current, *shard.shape)
    turned = sorted(range(len(sequence)), key=lambda place: sequence[len(sequence) - 1 - place])
    return pieces.transpose(*turned, *range(len(sequence), pieces.ndim)).reshape(-1, *shard.shape)


def gather_axes(shard, axes, sequence, dim):
    return laid_out(all_blocks(shard, axes, sequence), dim)


def in_blocks(shard, dim, peers):
    before, after = (shard.shape[:dim], shard.shape[dim + 1 :])
    return jnp.moveaxis(shard.reshape(*before, peers, -1, *after), dim, 0)


def summed_on_arrival(shard, axis, dim):
    pieces = in_blocks(shard, dim, lax.axis_size(axis))
    arrived = lax.all_to_all(pieces, axis, split_axis=0, concat_axis=0, tiled=True)
    return arrived.sum(axis=0)


def make_coeffs(inverses, pattern, delay, panel):
    half_panel = panel // 2
    positions = jnp.arange(panel, dtype=jnp.int32)
    active = (positions < panel - delay).astype(jnp.float32)
    active_lo = active[:half_panel]
    active_hi = active[half_panel:]
    diag_one = inverses[0] * active_lo
    off_diag = inverses[1] * pattern.astype(jnp.float32) * active_lo * active_hi
    diag_two = inverses[2] * active_hi
    return (diag_one, off_diag, diag_two)


def scale_pivots(columns, coeffs):
    diag_one, off_diag, diag_two = coeffs
    half_panel = diag_one.shape[0]
    left_half = columns[:, :half_panel]
    right_half = columns[:, half_panel:]
    return jnp.concatenate(
        [
            left_half * diag_one + right_half * off_diag,
            left_half * off_diag + right_half * diag_two,
        ],
        axis=1,
    )


def outer_update(left_rows, right_rows):
    return lax.dot_general(
        left_rows,
        right_rows,
        (((1,), (1,)), ((), ())),
        precision=lax.Precision.HIGHEST,
        preferred_element_type=jnp.float32,
    )


def local(old_tiles, remap, pivot_cols, pivot_order, pivot_pattern, block_inverses, delays):
    row_devices = lax.axis_size("row")
    col_devices = lax.axis_size(COL)
    peers = row_devices * col_devices
    row_index = lax.axis_index("row")
    col_index = lax.axis_index(COL)
    held = old_tiles.shape[1]
    tile_side = old_tiles.shape[2]
    panel = pivot_order.shape[2]
    rows_here = pivot_cols.shape[1]
    front_order = rows_here * peers
    contrib = front_order - 2 * panel
    tile_count = contrib // tile_side
    row_span = contrib // row_devices
    col_span = contrib // col_devices
    per_row = row_span // tile_side
    per_col = col_span // tile_side
    old_flat = old_tiles[0].reshape(held, tile_side * tile_side)
    targets = remap[0]
    tile_row = targets // tile_count
    tile_col = targets % tile_count
    owners = tile_row // per_row * col_devices + tile_col // per_col
    slots = tile_row % per_row * per_col + tile_col % per_col
    spread = min(peers, held // 2)
    capacity = (held + spread - 1) // spread
    indices = jnp.arange(held, dtype=jnp.int32)
    matched = (owners[:, None] == owners[None, :]) & (indices[None, :] < indices[:, None])
    ranks = jnp.sum(matched.astype(jnp.int32), axis=1)
    positions = owners * capacity + ranks
    places = peers * capacity
    routing = jnp.arange(places, dtype=jnp.int32)[:, None] == positions[None, :]
    outgoing = jnp.dot(
        routing.astype(jnp.bfloat16), old_flat, preferred_element_type=jnp.float32
    ).astype(jnp.bfloat16)
    labels = jnp.sum(jnp.where(routing, slots[None, :] + 1, 0), axis=1) - 1
    arrived, arrived_tags = (
        lax.all_to_all(outgoing, ROW_COL, split_axis=0, concat_axis=0, tiled=True),
        lax.all_to_all(labels, ROW_COL, split_axis=0, concat_axis=0, tiled=True),
    )
    slots_here = per_row * per_col
    collect = (jnp.arange(slots_here, dtype=jnp.int32)[:, None] == arrived_tags[None, :]).astype(
        jnp.bfloat16
    )
    summed = jnp.dot(collect, arrived, preferred_element_type=jnp.float32)
    front_c = (
        summed.reshape(per_row, per_col, tile_side, tile_side)
        .transpose(0, 2, 1, 3)
        .reshape(row_span, col_span)
    )
    orders = pivot_order[0]
    coeff_one = make_coeffs(block_inverses[0, 0], pivot_pattern[0, 0], delays[0, 0], panel)
    coeff_two = make_coeffs(block_inverses[0, 1], pivot_pattern[0, 1], delays[0, 1], panel)
    own_rows = pivot_cols[0]
    own_first = jnp.take(own_rows[:, :panel], orders[0], axis=1)
    own_second_raw = jnp.take(own_rows[:, panel:], orders[1], axis=1)
    own_start = (row_index * col_devices + col_index) * rows_here
    both_panels = gather_axes(
        jnp.concatenate([own_first, own_second_raw], axis=1), ROW_COL, (0, 2, 1), 0
    )
    first = both_panels[:, :panel].astype(jnp.float32)
    picked = jnp.take(first, panel + orders[1], axis=0)
    second = both_panels[:, panel:].astype(jnp.float32) - outer_update(
        scale_pivots(first, coeff_one), picked
    )
    own_second = lax.dynamic_slice_in_dim(second, own_start, rows_here, 0)
    pivot_span = 2 * panel
    row_first = scale_pivots(
        lax.dynamic_slice_in_dim(first, pivot_span + row_index * row_span, row_span, 0), coeff_one
    )
    row_second = scale_pivots(
        lax.dynamic_slice_in_dim(second, pivot_span + row_index * row_span, row_span, 0), coeff_two
    )
    col_first = lax.dynamic_slice_in_dim(first, pivot_span + col_index * col_span, col_span, 0)
    col_second = lax.dynamic_slice_in_dim(second, pivot_span + col_index * col_span, col_span, 0)
    parent = summed_on_arrival(
        front_c - outer_update(row_first, col_first) - outer_update(row_second, col_second),
        "team",
        0,
    )
    return (parent[None], own_second[None])


def solution(mesh):
    torus = Mesh(
        mesh.devices.reshape(mesh.shape["team"], mesh.shape["row"], 4, 4),
        ("team", "row", "col_0", "col_1"),
    )
    in_specs = (
        P("team", ROW_COL, None, None),
        P("team", ROW_COL),
        P("team", ROW_COL, None),
        P("team", None, None),
        P("team", None, None),
        P("team", None, None, None),
        P("team", None),
    )
    out_specs = (P("row", "team", COL), P("team", ROW_COL, None))
    return jax.shard_map(local, mesh=torus, in_specs=in_specs, out_specs=out_specs, check_vma=False)
```

profile of v0, /device:TPU:48, one launch (start us, length us, event | category | flops | bytes accessed | tf_op | source)
XLA Modules:
  0.0 439.0 jit_solution(3782700567953836906)
XLA Ops:
  7.2 0.0 all-gather.4.cloned.1.call-start
  7.2 0.8 fusion.45
  8.0 1.2 copy.18
  9.2 0.0 copy-start.8
  9.3 2.6 gather_fusion.2
  11.8 1.9 select_bitcast_fusion
  13.8 2.6 gather_fusion.1
  16.4 1.1 select_bitcast_fusion.1
  17.5 1.8 pad_maximum_fusion
  19.3 1.9 copy.19
  21.2 23.7 %all-gather = bf16[320,1024]{1,0:T(8,128)(2,1)} all-gather(bf16[160,1024]{1,0:T(8,128)(2,1)} %copy.19), channel_id=2, replica_groups=mesh['team'=8,'row'=2,'col_0'=4,'col_1'=4] {'row'}, dimensions={0}, use_global_device_ids=true | all-gather | bytes 983040 | tf_op jit(solution)/shard_map/all_gather | solution.py:20
  44.9 0.0 all-gather.4.cloned.1.call-update
  45.0 0.2 convert_reduce_fusion
  45.2 0.1 select_reduce_fusion
  45.3 0.7 sub.44
  46.0 8.4 %all-to-all-start = ((s32[32,2,1]{1,2,0:T(1,128)}), s32[32,2,1]{1,2,0:T(1,128)S(1)}, u32[]{:S(2)}, u32[]{:S(2)}) async-start(s32[32,2,1]{1,2,0:T(1,128)} %bitcast.5), calls=%async_computation | async-start | bytes 32768 | tf_op jit(solution)/shard_map/all_to_all | solution.py:115
  54.4 1.8 copy.21
  56.2 5.7 %convolution_convert_fusion = bf16[64,65536]{1,0:T(8,128)(2,1)} fusion(bf16[24,65536]{1,0:T(8,128)(2,1)S(1)} %bitcast.64, s32[24]{0:T(128)S(1)} %fusion.37), kind=kOutput, calls=%fused_computation.3 | convolution fusion | flops 205522432 | bytes 11534432 | tf_op jit(solution)/shard_map/dot_general | solution.py:109
  61.9 10.6 %all_to_all.16 = bf16[32,2,65536]{2,1,0:T(2,128)(2,1)} reshape(bf16[64,65536]{1,0:T(8,128)(2,1)} %convolution_convert_fusion) | data formatting | bytes 16777216 | tf_op jit(solution)/shard_map/all_to_all | solution.py:114
  72.6 10.0 %all-to-all-start.1 = ((bf16[32,2,65536]{2,1,0:T(2,128)(2,1)}), bf16[32,2,65536]{2,1,0:T(2,128)(2,1)}, u32[]{:S(2)}, u32[]{:S(2)}) async-start(bf16[32,2,65536]{2,1,0:T(2,128)(2,1)} %all_to_all.16), calls=%async_computation.1 | async-start | bytes 16777216 | tf_op jit(solution)/shard_map/all_to_all | solution.py:114
  82.6 0.2 all-gather.6.cloned.1.call-start
  82.8 73.6 %all-gather.4.cloned.1.call-done = bf16[8,160,1024]{2,1,0:T(8,128)(2,1)} async-done(((bf16[2,160,1024]{2,1,0:T(8,128)(2,1)}), bf16[8,160,1024]{2,1,0:T(8,128)(2,1)}) %all-gather.4.cloned.1.call-update) | async-done | bytes 2621456 | tf_op jit(solution)/shard_map/all_gather | solution.py:20
  156.4 0.0 all-gather.6.cloned.1.call-update
  156.5 0.6 fusion.46
  158.5 0.5 broadcast.309
  159.0 0.7 reduce.3
  159.7 0.1 eq.58
  159.8 132.2 %all-to-all-done.1 = bf16[32,2,65536]{2,1,0:T(2,128)(2,1)} async-done(((bf16[32,2,65536]{2,1,0:T(2,128)(2,1)}), bf16[32,2,65536]{2,1,0:T(2,128)(2,1)}, u32[]{:S(2)}, u32[]{:S(2)}) %all-to-all-start.1) | async-done | bytes 8388640 | tf_op jit(solution)/shard_map/all_to_all | solution.py:114
  292.0 10.3 %all_to_all.18 = bf16[64,65536]{1,0:T(8,128)(2,1)} reshape(bf16[32,2,65536]{2,1,0:T(2,128)(2,1)} %all-to-all-done.1) | data formatting | bytes 16777216 | tf_op jit(solution)/shard_map/all_to_all | solution.py:114
  302.3 4.6 %fusion.27 = f32[8,65536]{1,0:T(8,128)S(1)} fusion(bf16[64,65536]{1,0:T(8,128)(2,1)} %all_to_all.18, s32[64]{0:T(128)S(1)} %eq.58), kind=kOutput, calls=%fused_computation.48 | convolution fusion | flops 67109376 | bytes 10486016 | tf_op jit(solution)/shard_map/dot_general | solution.py:121
  306.9 1.6 reshape_transpose_reshape.3
  308.5 18.0 %all-gather.6.cloned.1.call-done = bf16[32,160,1024]{2,1,0:T(8,128)(2,1)} async-done(((bf16[8,160,1024]{2,1,0:T(8,128)(2,1)}), bf16[32,160,1024]{2,1,0:T(8,128)(2,1)}) %all-gather.6.cloned.1.call-update) | async-done | bytes 10485776 | tf_op jit(solution)/shard_map/all_gather | solution.py:20
  326.5 9.8 %copy.20 = bf16[2,4,4,160,1024]{4,3,2,1,0:T(8,128)(2,1)} copy(bf16[2,4,4,160,1024]{4,3,0,2,1:T(8,128)(2,1)} %bitcast.65) | data formatting | bytes 20971520 | tf_op jit(solution)/shard_map/transpose | solution.py:24
  336.3 10.0 %fusion.42 = (bf16[5120,512]{1,0:T(8,128)(2,1)}, f32[5120,512]{1,0:T(8,128)}) fusion(bf16[5120,1024]{1,0:T(8,128)(2,1)} %bitcast.60), kind=kLoop, calls=%fused_computation.99 | loop fusion | flops 2621440 | bytes 20971520 | tf_op jit(solution)/shard_map/slice | solution.py:137
  346.3 6.2 %gather_fusion = f32[512,512]{1,0:T(8,128)S(1)} fusion(f32[5120,512]{1,0:T(8,128)} %get-tuple-element.12, s32[1024]{0:T(1024)S(1)} %pad_clamp_fusion), kind=kCustom, calls=%fused_computation.2 | custom fusion | bytes 2099200 | tf_op jit(solution)/shard_map/jit(_take)/gather | solution.py:138
  352.5 0.0 slice-start.2
  352.5 9.2 %multiply_add_fusion.1 = (f32[5120,256]{1,0:T(8,128)}, f32[5120,256]{1,0:T(8,128)}) fusion(f32[5120,512]{1,0:T(8,128)} %get-tuple-element.12, f32[256]{0:T(256)S(1)} %get-tuple-element.32, f32[256]{0:T(256)S(1)} %get-tuple-element.30, f32[256]{0:T(256)S(1)} %get-tuple-element.31), kind=kLoop, calls=%fused_computation.10 | loop fusion | flops 7864320 | bytes 20974592 | tf_op jit(solution)/shard_map/add | solution.py:61
  361.7 2.8 multiply_add_fusion.5
  364.5 0.9 copy-done.1
  365.4 20.4 %convert_subtract_fusion = f32[5120,512]{1,0:T(8,128)S(1)} fusion(f32[5120,256]{1,0:T(8,128)} %get-tuple-element.8, f32[5120,256]{1,0:T(8,128)S(1)} %copy-done.1, bf16[5120,1024]{1,0:T(8,128)(2,1)S(1)} %bitcast.63, f32[512,512]{1,0:T(8,128)S(1)} %gather_fusion, pred[512]{0:T(512)(128)(4,1)S(1)} %get-tuple-element.28), kind=kOutput, calls=%fused_computation.8 | convolution fusion | flops 16114253824 | bytes 27263488 | tf_op jit(solution)/shard_map/dot_general | solution.py:69
  385.8 0.6 multiply_add_fusion.3
  386.4 2.6 copy-done.2
  389.0 3.4 fusion.17
  392.4 5.0 %fusion.14 = f32[2048,256]{1,0:T(8,128)} fusion(f32[2048,256]{1,0:T(8,128)S(1)} %fusion.17, f32[2048,256]{1,0:T(8,128)S(1)} %get-tuple-element.6, f32[2048,256]{1,0:T(8,128)S(1)} %get-tuple-element.5, f32[5120,512]{1,0:T(8,128)S(1)} %convert_subtract_fusion, s32[]{:T(128)S(6)} %select_n.109), kind=kOutput, calls=%fused_computation.19 | convolution fusion | flops 3222798336 | bytes 8912900 | tf_op jit(solution)/shard_map/dot_general | solution.py:69
  397.4 6.8 %all-to-all-start.2 = ((f32[8,256,256]{2,1,0:T(8,128)}), f32[8,256,256]{2,1,0:T(8,128)S(1)}, u32[]{:S(2)}, u32[]{:S(2)}) async-start(f32[8,256,256]{2,1,0:T(8,128)} %bitcast.28), calls=%async_computation.2 | async-start | bytes 4194304 | tf_op jit(solution)/shard_map/all_to_all | solution.py:38
  404.2 1.7 dynamic-slice_bitcast_fusion
  405.9 25.5 %all-to-all-done.2 = f32[8,256,256]{2,1,0:T(8,128)S(1)} async-done(((f32[8,256,256]{2,1,0:T(8,128)}), f32[8,256,256]{2,1,0:T(8,128)S(1)}, u32[]{:S(2)}, u32[]{:S(2)}) %all-to-all-start.2) | async-done | bytes 2097184 | tf_op jit(solution)/shard_map/all_to_all | solution.py:38
  431.3 0.8 reduce_sum.32
  (40 shorter events, 0.2 us)
Async XLA Ops:
  7.2 149.3 %all-gather.4.cloned.1.call-start = ((), (), s32[]{:S(2)}) async-start(), calls=%async_computation.3 | async-start | bytes 3276800 | tf_op jit(solution)/shard_map/all_gather | solution.py:20
  9.2 35.7 %copy-start.8 = (s32[1,24]{1,0:T(1,128)S(1)}, s32[1,24]{1,0:T(1,128)}, u32[]{:S(2)}) copy-start(s32[1,24]{1,0:T(1,128)} %param.10) | copy-start | bytes 292
  11.8 42.6 %copy-start.3 = (bf16[1,24,256,256]{3,2,1,0:T(8,128)(2,1)S(1)}, bf16[1,24,256,256]{3,2,1,0:T(8,128)(2,1)}, u32[]{:S(2)}) copy-start(bf16[1,24,256,256]{3,2,1,0:T(8,128)(2,1)} %param.9) | copy-start | bytes 9437188
  46.0 26.5 %all-to-all-start = ((s32[32,2,1]{1,2,0:T(1,128)}), s32[32,2,1]{1,2,0:T(1,128)S(1)}, u32[]{:S(2)}, u32[]{:S(2)}) async-start(s32[32,2,1]{1,2,0:T(1,128)} %bitcast.5), calls=%async_computation | async-start | bytes 32768 | tf_op jit(solution)/shard_map/all_to_all | solution.py:115
  72.5 83.9 %copy-start.7 = (s32[1,2]{1,0:T(1,128)S(1)}, s32[1,2]{1,0:T(1,128)}, u32[]{:S(2)}) copy-start(s32[1,2]{1,0:T(1,128)} %param.15) | copy-start | bytes 28
  72.5 85.8 %copy-start.4 = (s32[1,2,512]{2,1,0:T(2,128)S(1)}, s32[1,2,512]{2,1,0:T(2,128)}, u32[]{:S(2)}) copy-start(s32[1,2,512]{2,1,0:T(2,128)} %param.12) | copy-start | bytes 12292
  72.5 85.9 %copy-start.6 = (s32[1,2,256]{2,1,0:T(2,128)S(1)}, s32[1,2,256]{2,1,0:T(2,128)}, u32[]{:S(2)}) copy-start(s32[1,2,256]{2,1,0:T(2,128)} %param.13) | copy-start | bytes 6148
  72.5 85.9 %copy-start.5 = (f32[1,2,3,256]{3,1,2,0:T(2,128)S(1)}, f32[1,2,3,256]{3,1,2,0:T(2,128)}, u32[]{:S(2)}) copy-start(f32[1,2,3,256]{3,1,2,0:T(2,128)} %param.14) | copy-start | bytes 18436
  72.6 219.4 %all-to-all-start.1 = ((bf16[32,2,65536]{2,1,0:T(2,128)(2,1)}), bf16[32,2,65536]{2,1,0:T(2,128)(2,1)}, u32[]{:S(2)}, u32[]{:S(2)}) async-start(bf16[32,2,65536]{2,1,0:T(2,128)(2,1)} %all_to_all.16), calls=%async_computation.1 | async-start | bytes 16777216 | tf_op jit(solution)/shard_map/all_to_all | solution.py:114
  82.6 243.9 %all-gather.6.cloned.1.call-start = ((), (), s32[]{:S(2)}) async-start(), calls=%async_computation.4 | async-start | bytes 13107200 | tf_op jit(solution)/shard_map/all_gather | solution.py:20
  346.3 18.2 %slice-start = ((s8[10485760]{0:T(1024)(128)(4,1)}), s8[2097152]{0:T(1024)(128)(4,1)S(1)}, s32[]{:S(2)}) async-start(s8[10485760]{0:T(1024)(128)(4,1)} %bitcast.61), calls=%async_computation.5 | async-start | bytes 4194304
  352.5 12.0 %slice-start.1 = ((s8[10485760]{0:T(1024)(128)(4,1)}), s8[4194304]{0:T(1024)(128)(4,1)S(1)}, s32[]{:S(2)}) async-start(s8[10485760]{0:T(1024)(128)(4,1)} %bitcast.61), calls=%async_computation.6 | async-start | bytes 8388608
  352.5 12.0 %slice-start.2 = ((s8[10485760]{0:T(1024)(128)(4,1)}), s8[4194304]{0:T(1024)(128)(4,1)S(1)}, s32[]{:S(2)}) async-start(s8[10485760]{0:T(1024)(128)(4,1)} %bitcast.61), calls=%async_computation.7 | async-start | bytes 8388608
  361.6 3.7 copy-start.1
  385.8 6.6 %copy-start = (f32[5120,512]{1,0:T(8,128)}, f32[5120,512]{1,0:T(8,128)S(1)}, u32[]{:S(2)}) copy-start(f32[5120,512]{1,0:T(8,128)S(1)} %convert_subtract_fusion) | copy-start | bytes 31457284
  385.8 3.2 copy-start.2
  397.4 34.0 %all-to-all-start.2 = ((f32[8,256,256]{2,1,0:T(8,128)}), f32[8,256,256]{2,1,0:T(8,128)S(1)}, u32[]{:S(2)}, u32[]{:S(2)}) async-start(f32[8,256,256]{2,1,0:T(8,128)} %bitcast.28), calls=%async_computation.2 | async-start | bytes 4194304 | tf_op jit(solution)/shard_map/all_to_all | solution.py:38
Sparse Core Ops, SparseCore 0:
  45.0 111.3 all-gather.3
  158.2 168.2 all-gather.5
where the time goes:
time: 440 us; the launch traced here: 439 us
  waiting for transfers between devices  249 us (57%)
  local copies, waits for them, and re-layouts  56.5 us (13%)
  matrix products  39.1 us (9%)
  other arithmetic  29.3 us (7%)
  starting transfers between devices  25.5 us (6%)
  blocking collectives  23.7 us (5%)
  between operations  15.7 us (4%)
    all_to_all x1, waiting for transfers between devices, local(): lax.all_to_all(outgoing, ROW_COL, split_axis=0, concat_axis=0, tiled=True)  132 us
    all_gather x2, waiting for transfers between devices, all_blocks(): pieces = lax.all_gather(pieces, axes[k], axis=0, tiled=True)  91.6 us
    dot_general x3, matrix products, outer_update(): lax.dot_general(left_rows, right_rows, (((1,), (1,)), ((), ())), precisio...  28.8 us
    all_to_all x1, waiting for transfers between devices, summed_on_arrival(): lax.all_to_all(pieces, axis, split_axis=0, concat_axis=0, tiled=True)  25.5 us
    all_gather x1, blocking collectives, all_blocks(): pieces = lax.all_gather(pieces, axes[k], axis=0, tiled=True)  23.7 us
    all_to_all x2, local copies, waits for them, and re-layouts, local(): lax.all_to_all(outgoing, ROW_COL, split_axis=0, concat_axis=0, tiled=True)  20.9 us
    add x3, other arithmetic, scale_pivots(): left_half * diag_one + right_half * off_diag  12.5 us
    all_to_all x1, starting transfers between devices, local(): lax.all_to_all(outgoing, ROW_COL, split_axis=0, concat_axis=0, tiled=True)  10 us
  transfers between devices with their start and end apart: 5, of which 4 were waited for; matrix products, arithmetic and copies ran while one was open for 4% of the time, Pallas kernels for 0%

commit v1 on v0

--- a/solution.py
+++ b/solution.py
@@ -17,7 +17,8 @@
 def all_blocks(shard, axes, sequence):
     pieces = shard[None]
     for k in sequence:
-        pieces = lax.all_gather(pieces, axes[k], axis=0, tiled=True)
+        sent = jnp.stack([pieces] * lax.axis_size(axes[k]))
+        pieces = jnp.concatenate(lax.all_to_all(sent, axes[k], 0, 0), axis=0)
     current = [lax.axis_size(axes[k]) for k in reversed(sequence)]
     pieces = pieces.reshape(*current, *shard.shape)
     turned = sorted(range(len(sequence)), key=lambda place: sequence[len(sequence) - 1 - place])

time: 440 us -> 502 us (1.14); the launches traced: 439 us -> 494 us
  blocking collectives: 23.7 us -> 86.1 us
  between operations: 15.7 us -> 2.28 us
  waiting for transfers between devices: 249 us -> 240 us
  starting transfers between devices: 25.5 us -> 31.5 us
    all_to_all x0 -> x1, waiting for transfers between devices: none -> 94.4 us  [all_blocks(): pieces = jnp.concatenate(lax.all_to_all(sent, axes[k], 0, 0), axis=0)]
    all_gather x2 -> x0, waiting for transfers between devices: 91.6 us -> none  [all_blocks(): pieces = lax.all_gather(pieces, axes[k], axis=0, tiled=True)]
    all_to_all x0 -> x2, blocking collectives: none -> 86.1 us  [all_blocks(): pieces = jnp.concatenate(lax.all_to_all(sent, axes[k], 0, 0), axis=0)]
    all_gather x1 -> x0, blocking collectives: 23.7 us -> none  [all_blocks(): pieces = lax.all_gather(pieces, axes[k], axis=0, tiled=True)]
    all_to_all x1, waiting for transfers between devices: 132 us -> 120 us  [local(): lax.all_to_all(outgoing, ROW_COL, split_axis=0, concat_axis=0, tiled=True)]
    all_to_all x0 -> x1, starting transfers between devices: none -> 6.83 us  [all_blocks(): pieces = jnp.concatenate(lax.all_to_all(sent, axes[k], 0, 0), axis=0)]
    another operation x0 -> x3, local copies, waits for them, and re-layouts: none -> 6.21 us  [all_blocks(): sent = jnp.stack([pieces] * lax.axis_size(axes[k]))]
  transfers between devices with their start and end apart: 5 -> 4, of which waited for: 4 -> 3; matrix products, arithmetic and copies ran while one was open for 4% -> 17% of each run, Pallas kernels for 0% -> 0%
where the time goes in v1:
time: 502 us; the launch traced here: 494 us
  waiting for transfers between devices  240 us (48%)
  blocking collectives  86.1 us (17%)
  local copies, waits for them, and re-layouts  60.2 us (12%)
  matrix products  43.5 us (9%)
  starting transfers between devices  31.5 us (6%)
  other arithmetic  30.8 us (6%)
    all_to_all x1, waiting for transfers between devices, local(): lax.all_to_all(outgoing, ROW_COL, split_axis=0, concat_axis=0, tiled=True)  120 us
    all_to_all x1, waiting for transfers between devices, all_blocks(): pieces = jnp.concatenate(lax.all_to_all(sent, axes[k], 0, 0), axis=0)  94.4 us
    all_to_all x2, blocking collectives, all_blocks(): pieces = jnp.concatenate(lax.all_to_all(sent, axes[k], 0, 0), axis=0)  86.1 us
    dot_general x3, matrix products, outer_update(): lax.dot_general(left_rows, right_rows, (((1,), (1,)), ((), ())), precisio...  31.7 us
    all_to_all x1, waiting for transfers between devices, summed_on_arrival(): lax.all_to_all(pieces, axis, split_axis=0, concat_axis=0, tiled=True)  25.5 us
    all_to_all x2, local copies, waits for them, and re-layouts, local(): lax.all_to_all(outgoing, ROW_COL, split_axis=0, concat_axis=0, tiled=True)  20.8 us
    add x3, other arithmetic, scale_pivots(): left_half * diag_one + right_half * off_diag  16.6 us
    all_to_all x1, starting transfers between devices, local(): lax.all_to_all(labels, ROW_COL, split_axis=0, concat_axis=0, tiled=True)  11.1 us
  transfers between devices with their start and end apart: 4, of which 3 were waited for; matrix products, arithmetic and copies ran while one was open for 17% of the time, Pallas kernels for 0%

profile of v1, /device:TPU:48, one launch (start us, length us, event | category | flops | bytes accessed | tf_op | source)
XLA Modules:
  0.0 494.1 jit_solution(8017353610093166720)
XLA Ops:
  0.6 0.7 fusion.36
  1.3 0.7 fusion.34
  2.0 0.7 fusion.33
  2.6 0.2 convert_reduce_fusion
  2.8 0.1 select_reduce_fusion
  2.9 0.7 sub.44
  3.7 11.1 %all-to-all-start = ((s32[32,2,1]{1,2,0:T(1,128)}), s32[32,2,1]{1,2,0:T(1,128)S(1)}, u32[]{:S(2)}, u32[]{:S(2)}) async-start(s32[32,2,1]{1,2,0:T(1,128)} %bitcast.5), calls=%async_computation | async-start | bytes 32768 | tf_op jit(solution)/shard_map/all_to_all | solution.py:116
  14.8 0.8 fusion.45
  15.6 1.2 copy.19
  16.8 2.0 gather_fusion.2
  18.8 0.1 select_bitcast_fusion
  18.9 2.0 gather_fusion.1
  20.9 0.1 select_bitcast_fusion.1
  21.1 0.1 maximum_bitcast_fusion
  21.2 0.2 pad_maximum_fusion
  21.4 0.5 copy.20
  21.8 25.3 %all_to_all.38 = bf16[2,1,160,1024]{3,2,1,0:T(8,128)(2,1)S(1)} all-to-all(bf16[2,1,160,1024]{3,2,1,0:T(8,128)(2,1)S(1)} %copy.20), channel_id=1, replica_groups=mesh['team'=8,'row'=2,'col_0'=4,'col_1'=4] {'row'}, dimensions={0} | all-to-all | bytes 1310720 | tf_op jit(solution)/shard_map/all_to_all | solution.py:21
  47.1 0.3 stack.10
  47.4 60.9 %all_to_all.39 = bf16[4,2,160,1024]{3,2,1,0:T(8,128)(2,1)S(1)} all-to-all(bf16[4,2,160,1024]{3,2,1,0:T(8,128)(2,1)S(1)} %stack.10), channel_id=1, replica_groups=mesh['team'=8,'row'=2,'col_0'=4,'col_1'=4] {'col_1'}, dimensions={0} | all-to-all | bytes 5242880 | tf_op jit(solution)/shard_map/all_to_all | solution.py:21
  108.3 5.4 %stack.11 = bf16[4,8,160,1024]{3,2,1,0:T(8,128)(2,1)} broadcast(bf16[8,160,1024]{2,1,0:T(8,128)(2,1)S(1)} %bitcast.68), dimensions={1,2,3} | broadcast | bytes 13107200 | tf_op jit(solution)/shard_map/stack | solution.py:20
  113.7 6.8 %all-to-all-start.4 = ((bf16[4,8,160,1024]{3,2,1,0:T(8,128)(2,1)}), bf16[4,8,160,1024]{3,2,1,0:T(8,128)(2,1)}, u32[]{:S(2)}, u32[]{:S(2)}) async-start(bf16[4,8,160,1024]{3,2,1,0:T(8,128)(2,1)} %stack.11), calls=%async_computation.4 | async-start | bytes 20971520 | tf_op jit(solution)/shard_map/all_to_all | solution.py:21
  120.6 1.8 copy.22
  122.3 5.8 %convolution_convert_fusion = bf16[64,65536]{1,0:T(8,128)(2,1)} fusion(bf16[24,65536]{1,0:T(8,128)(2,1)S(1)} %bitcast.67, s32[24]{0:T(128)S(1)} %fusion.37), kind=kOutput, calls=%fused_computation.3 | convolution fusion | flops 205522432 | bytes 11534432 | tf_op jit(solution)/shard_map/dot_general | solution.py:110
  128.2 10.6 %all_to_all.25 = bf16[32,2,65536]{2,1,0:T(2,128)(2,1)} reshape(bf16[64,65536]{1,0:T(8,128)(2,1)} %convolution_convert_fusion) | data formatting | bytes 16777216 | tf_op jit(solution)/shard_map/all_to_all | solution.py:115
  138.7 94.4 %all-to-all-done.4 = bf16[4,8,160,1024]{3,2,1,0:T(8,128)(2,1)} async-done(((bf16[4,8,160,1024]{3,2,1,0:T(8,128)(2,1)}), bf16[4,8,160,1024]{3,2,1,0:T(8,128)(2,1)}, u32[]{:S(2)}, u32[]{:S(2)}) %all-to-all-start.4) | async-done | bytes 10485792 | tf_op jit(solution)/shard_map/all_to_all | solution.py:21
  233.1 9.2 %all-to-all-start.1 = ((bf16[32,2,65536]{2,1,0:T(2,128)(2,1)}), bf16[32,2,65536]{2,1,0:T(2,128)(2,1)}, u32[]{:S(2)}, u32[]{:S(2)}) async-start(bf16[32,2,65536]{2,1,0:T(2,128)(2,1)} %all_to_all.25), calls=%async_computation.1 | async-start | bytes 16777216 | tf_op jit(solution)/shard_map/all_to_all | solution.py:115
  242.4 0.6 fusion.46
  244.4 0.5 broadcast.311
  244.9 0.7 reduce.3
  245.6 0.1 eq.58
  245.7 10.0 %copy.21 = bf16[2,4,4,160,1024]{4,3,2,1,0:T(8,128)(2,1)} copy(bf16[2,4,4,160,1024]{4,3,0,2,1:T(8,128)(2,1)} %bitcast.15) | data formatting | bytes 20971520 | tf_op jit(solution)/shard_map/transpose | solution.py:25
  255.7 9.7 %fusion.42 = (bf16[5120,512]{1,0:T(8,128)(2,1)}, f32[5120,512]{1,0:T(8,128)}) fusion(bf16[5120,1024]{1,0:T(8,128)(2,1)} %bitcast.63), kind=kLoop, calls=%fused_computation.100 | loop fusion | flops 2621440 | bytes 20971520 | tf_op jit(solution)/shard_map/slice | solution.py:138
  265.5 6.0 %gather_fusion = f32[512,512]{1,0:T(8,128)S(1)} fusion(f32[5120,512]{1,0:T(8,128)} %get-tuple-element.12, s32[1024]{0:T(1024)S(1)} %pad_clamp_fusion), kind=kCustom, calls=%fused_computation.2 | custom fusion | bytes 2099200 | tf_op jit(solution)/shard_map/jit(_take)/gather | solution.py:139
  271.5 4.8 multiply_add_fusion.5
  276.3 9.3 %multiply_add_fusion.1 = (f32[5120,256]{1,0:T(8,128)}, f32[5120,256]{1,0:T(8,128)}) fusion(f32[5120,512]{1,0:T(8,128)} %get-tuple-element.12, f32[256]{0:T(256)S(1)} %get-tuple-element.32, f32[256]{0:T(256)S(1)} %get-tuple-element.30, f32[256]{0:T(256)S(1)} %get-tuple-element.31), kind=kLoop, calls=%fused_computation.10 | loop fusion | flops 7864320 | bytes 20974592 | tf_op jit(solution)/shard_map/add | solution.py:62
  285.6 21.1 %convert_subtract_fusion = f32[5120,512]{1,0:T(8,128)S(1)} fusion(f32[5120,256]{1,0:T(8,128)} %get-tuple-element.8, f32[5120,256]{1,0:T(8,128)} %get-tuple-element.7, bf16[5120,1024]{1,0:T(8,128)(2,1)S(1)} %bitcast.66, f32[512,512]{1,0:T(8,128)S(1)} %gather_fusion, pred[512]{0:T(512)(128)(4,1)S(1)} %get-tuple-element.28), kind=kOutput, calls=%fused_computation.8 | convolution fusion | flops 16114253824 | bytes 27263488 | tf_op jit(solution)/shard_map/dot_general | solution.py:70
  306.7 4.0 copy-done
  310.7 2.5 multiply_add_fusion.3
  313.3 119.9 %all-to-all-done.1 = bf16[32,2,65536]{2,1,0:T(2,128)(2,1)} async-done(((bf16[32,2,65536]{2,1,0:T(2,128)(2,1)}), bf16[32,2,65536]{2,1,0:T(2,128)(2,1)}, u32[]{:S(2)}, u32[]{:S(2)}) %all-to-all-start.1) | async-done | bytes 8388640 | tf_op jit(solution)/shard_map/all_to_all | solution.py:115
  433.1 10.2 %all_to_all.27 = bf16[64,65536]{1,0:T(8,128)(2,1)} reshape(bf16[32,2,65536]{2,1,0:T(2,128)(2,1)} %all-to-all-done.1) | data formatting | bytes 16777216 | tf_op jit(solution)/shard_map/all_to_all | solution.py:115
  443.3 6.0 %fusion.27 = f32[8,65536]{1,0:T(8,128)} fusion(bf16[64,65536]{1,0:T(8,128)(2,1)} %all_to_all.27, s32[64]{0:T(128)S(1)} %eq.58), kind=kOutput, calls=%fused_computation.49 | convolution fusion | flops 67109376 | bytes 10486016 | tf_op jit(solution)/shard_map/dot_general | solution.py:122
  449.3 1.9 reshape_transpose_reshape.3
  451.2 4.6 fusion.17
  455.8 6.0 %fusion.14 = f32[2048,256]{1,0:T(8,128)} fusion(f32[2048,256]{1,0:T(8,128)S(1)} %fusion.17, f32[2048,256]{1,0:T(8,128)S(1)} %copy-done.2, f32[2048,256]{1,0:T(8,128)S(1)} %copy-done.1, f32[5120,512]{1,0:T(8,128)} %copy-done, s32[]{:T(128)S(6)} %select_n.109), kind=kOutput, calls=%fused_computation.19 | convolution fusion | flops 3222798336 | bytes 8912900 | tf_op jit(solution)/shard_map/dot_general | solution.py:70
  461.8 4.3 all-to-all-start.5
  466.1 1.7 dynamic-slice_bitcast_fusion
  467.8 25.5 %all-to-all-done.5 = f32[8,256,256]{2,1,0:T(8,128)S(1)} async-done(((f32[8,256,256]{2,1,0:T(8,128)}), f32[8,256,256]{2,1,0:T(8,128)S(1)}, u32[]{:S(2)}, u32[]{:S(2)}) %all-to-all-start.5) | async-done | bytes 2097184 | tf_op jit(solution)/shard_map/all_to_all | solution.py:39
  493.2 0.8 reduce_sum.32
  (38 shorter events, 0.2 us)
Async XLA Ops:
  3.7 18.2 %all-to-all-start = ((s32[32,2,1]{1,2,0:T(1,128)}), s32[32,2,1]{1,2,0:T(1,128)S(1)}, u32[]{:S(2)}, u32[]{:S(2)}) async-start(s32[32,2,1]{1,2,0:T(1,128)} %bitcast.5), calls=%async_computation | async-start | bytes 32768 | tf_op jit(solution)/shard_map/all_to_all | solution.py:116
  113.7 6.8 %copy-start.3 = (bf16[1,24,256,256]{3,2,1,0:T(8,128)(2,1)S(1)}, bf16[1,24,256,256]{3,2,1,0:T(8,128)(2,1)}, u32[]{:S(2)}) copy-start(bf16[1,24,256,256]{3,2,1,0:T(8,128)(2,1)} %param.9) | copy-start | bytes 9437188
  113.7 119.4 %all-to-all-start.4 = ((bf16[4,8,160,1024]{3,2,1,0:T(8,128)(2,1)}), bf16[4,8,160,1024]{3,2,1,0:T(8,128)(2,1)}, u32[]{:S(2)}, u32[]{:S(2)}) async-start(bf16[4,8,160,1024]{3,2,1,0:T(8,128)(2,1)} %stack.11), calls=%async_computation.4 | async-start | bytes 20971520 | tf_op jit(solution)/shard_map/all_to_all | solution.py:21
  138.7 103.6 %copy-start.7 = (s32[1,2]{1,0:T(1,128)S(1)}, s32[1,2]{1,0:T(1,128)}, u32[]{:S(2)}) copy-start(s32[1,2]{1,0:T(1,128)} %param.15) | copy-start | bytes 28
  138.7 105.6 %copy-start.4 = (s32[1,2,512]{2,1,0:T(2,128)S(1)}, s32[1,2,512]{2,1,0:T(2,128)}, u32[]{:S(2)}) copy-start(s32[1,2,512]{2,1,0:T(2,128)} %param.12) | copy-start | bytes 12292
  138.7 105.6 %copy-start.6 = (s32[1,2,256]{2,1,0:T(2,128)S(1)}, s32[1,2,256]{2,1,0:T(2,128)}, u32[]{:S(2)}) copy-start(s32[1,2,256]{2,1,0:T(2,128)} %param.13) | copy-start | bytes 6148
  138.7 105.6 %copy-start.5 = (f32[1,2,3,256]{3,1,2,0:T(2,128)S(1)}, f32[1,2,3,256]{3,1,2,0:T(2,128)}, u32[]{:S(2)}) copy-start(f32[1,2,3,256]{3,1,2,0:T(2,128)} %param.14) | copy-start | bytes 18436
  233.1 200.0 %all-to-all-start.1 = ((bf16[32,2,65536]{2,1,0:T(2,128)(2,1)}), bf16[32,2,65536]{2,1,0:T(2,128)(2,1)}, u32[]{:S(2)}, u32[]{:S(2)}) async-start(bf16[32,2,65536]{2,1,0:T(2,128)(2,1)} %all_to_all.25), calls=%async_computation.1 | async-start | bytes 16777216 | tf_op jit(solution)/shard_map/all_to_all | solution.py:115
  271.5 14.1 %slice-start = ((s8[10485760]{0:T(1024)(128)(4,1)}), s8[4194304]{0:T(1024)(128)(4,1)S(1)}, s32[]{:S(2)}) async-start(s8[10485760]{0:T(1024)(128)(4,1)} %bitcast.64), calls=%async_computation.6 | async-start | bytes 8388608
  276.3 9.3 %slice-start.1 = ((s8[10485760]{0:T(1024)(128)(4,1)}), s8[4194304]{0:T(1024)(128)(4,1)S(1)}, s32[]{:S(2)}) async-start(s8[10485760]{0:T(1024)(128)(4,1)} %bitcast.64), calls=%async_computation.7 | async-start | bytes 8388608
  276.3 9.3 %slice-start.2 = ((s8[10485760]{0:T(1024)(128)(4,1)}), s8[2097152]{0:T(1024)(128)(4,1)S(1)}, s32[]{:S(2)}) async-start(s8[10485760]{0:T(1024)(128)(4,1)} %bitcast.64), calls=%async_computation.8 | async-start | bytes 4194304
  306.7 4.0 copy-start
  451.2 4.6 copy-start.1
  451.2 4.6 copy-start.2
  461.8 31.5 %all-to-all-start.5 = ((f32[8,256,256]{2,1,0:T(8,128)}), f32[8,256,256]{2,1,0:T(8,128)S(1)}, u32[]{:S(2)}, u32[]{:S(2)}) async-start(f32[8,256,256]{2,1,0:T(8,128)} %bitcast.30), calls=%async_computation.5 | async-start | bytes 4194304 | tf_op jit(solution)/shard_map/all_to_all | solution.py:39
